TPU v7x, 32 devices: a whole 2x2x4 slice. The times are simulated.
32 devices in a mesh: tok: 8 (over y, x, core), layer: 4 (over z).
Axes of the slice: x: 2, y: 2, z: 4, core: 2. Of those that a mesh axis runs over, the one named last changes fastest.
Arguments:
- activations: bfloat16 [4, 896, 5120], P(None, ('tok', 'layer')), may hold values from -9 to 9
- pos_weight: bfloat16 [4, 48, 5120], P('layer', None, 'tok'), may hold values from -1 to 1
- depth_weight: bfloat16 [4, 128, 5120], P('layer', None, 'tok'), may hold values from -0.01953125 to 0.01953125
- tags: int32 [896], P(('tok', 'layer')), may hold values from 0 to 47
- depths: int32 [896], P(('tok', 'layer')), may hold values from 2 to 14
- counts: int32 [32], P(('tok', 'layer')), may hold values from 1 to 28, 560 in all
Outputs:
- pos_grad: float32 [4, 48, 5120], P('layer', None, 'tok')
- depth_grad: float32 [4, 128, 5120], P('layer', None, 'tok')
Inputs may be any that keep to these rules, and one draw needn't show every extreme that they name: counts[d] is the number of live slots among device d's 28 slots, which are its first ones; the largest count equals 28.
All inputs are finite; a program needn't handle non-finite values.
Results may differ from a plain program's by a relative error of at most 0.0042.
Values may be sent and summed in bfloat16 or wider, within the bound.
No kernel may reach another device: no remote copies, remote signals or barrier semaphores. Data moves between devices by JAX's collectives and lax.ppermute only.
A program may use at most 64 MiB of HBM per device.

v0:
```python
import jax
import jax.numpy as jnp
from jax import lax
from jax.sharding import PartitionSpec as P


def contract(left, right):
    return lax.dot_general(
        left, right, (((1,), (1,)), ((), ())), preferred_element_type=jnp.float32
    )


def local(activations, pos_weight, depth_weight, tags, depths, counts):
    tag_count = pos_weight.shape[1]
    slots_each = tags.shape[0]
    owned_rows = lax.all_to_all(activations, "layer", split_axis=0, concat_axis=1, tiled=True)[0]
    row_count = owned_rows.shape[0]
    pos_full, depth_full = (
        lax.all_gather(pos_weight, "tok", axis=2, tiled=True),
        lax.all_gather(depth_weight, "tok", axis=2, tiled=True),
    )
    logits = contract(owned_rows, pos_full[0])
    hidden = contract(owned_rows, depth_full[0])
    tag_rows, depth_rows, block_counts = (
        lax.all_gather(tags, "layer", axis=0, tiled=True),
        lax.all_gather(depths, "layer", axis=0, tiled=True),
        lax.all_gather(counts, "layer", axis=0, tiled=True),
    )
    row_count = owned_rows.shape[0]
    slot_index = jnp.arange(row_count, dtype=jnp.int32)
    position = slot_index % slots_each
    block_index = slot_index // slots_each
    source_index = jnp.arange(block_counts.shape[0], dtype=jnp.int32)
    match = block_index[:, None] == source_index[None, :]
    block_count = jnp.sum(jnp.where(match, block_counts[None, :], 0), axis=1)
    live = position < block_count
    token_scale = jnp.where(live, 1.0 / block_count.astype(jnp.float32), jnp.float32(0.0))
    top = jnp.max(logits, axis=1, keepdims=True)
    expo = jnp.exp(logits - top)
    probabilities = expo / jnp.sum(expo, axis=1, keepdims=True)
    onehot = (tag_rows[:, None] == jnp.arange(tag_count, dtype=jnp.int32)[None, :]).astype(
        jnp.float32
    )
    g_pos = (probabilities - onehot) * token_scale[:, None]
    predicted = jnp.sum(hidden * hidden, axis=1)
    residual = predicted - depth_rows.astype(jnp.float32)
    g_depth = hidden * (residual * token_scale)[:, None]
    joined = jnp.concatenate([g_pos, g_depth], axis=1).astype(jnp.bfloat16)
    partial_value = lax.dot_general(
        joined, owned_rows, (((0,), (0,)), ((), ())), preferred_element_type=jnp.float32
    )
    summed = lax.psum_scatter(partial_value, "tok", scatter_dimension=1, tiled=True)
    return (summed[None, :tag_count], summed[None, tag_count:])


def solution(mesh):
    in_specs = (
        P(None, ("tok", "layer"), None),
        P("layer", None, "tok"),
        P("layer", None, "tok"),
        P(("tok", "layer")),
        P(("tok", "layer")),
        P(("tok", "layer")),
    )
    out_specs = (P("layer", None, "tok"), P("layer", None, "tok"))
    return jax.shard_map(local, mesh=mesh, in_specs=in_specs, out_specs=out_specs, check_vma=False)
```

profile of v0, /device:TPU:0, one launch (start us, length us, event | category | flops | bytes accessed | tf_op | source)
XLA Modules:
  0.0 121.3 jit_solution(3558480819830327647)
XLA Ops:
  7.2 0.0 all-gather.2.cloned.1.call-start
  7.2 0.7 all-gather.2.cloned.1.call-update
  7.9 2.7 %copy.13 = bf16[4,28,5120]{2,1,0:T(8,128)(2,1)} copy(bf16[4,28,5120]{2,0,1:T(4,128)(2,1)} %param.6) | data formatting | bytes 2293760 | tf_op args[0]
  10.6 0.0 copy-start.3
  10.6 0.0 copy-start.1
  10.6 0.0 copy-start.2
  10.6 0.0 copy-start
  10.6 6.5 %all-to-all-start = ((bf16[4,28,5120]{2,1,0:T(8,128)(2,1)}), bf16[4,28,5120]{2,1,0:T(8,128)(2,1)S(1)}, u32[]{:S(2)}, u32[]{:S(2)}) async-start(bf16[4,28,5120]{2,1,0:T(8,128)(2,1)} %copy.13), calls=%async_computation | async-start | bytes 2621440 | tf_op jit(solution)/shard_map/all_to_all | solution.py:16
  17.1 0.0 reduce-scatter.2.cloned.1.call-start
  17.8 0.0 copy-done.3
  17.8 0.6 dynamic-slice
  19.0 0.0 copy-done.1
  19.0 0.2 dynamic-update-slice.2
  19.3 0.0 copy-done.2
  19.3 0.2 dynamic-update-slice
  19.5 0.8 dynamic-update-slice.1
  20.3 28.4 %all-reduce.3 = (s32[4]{0:T(128)S(1)}, s32[112]{0:T(128)S(1)}, s32[112]{0:T(128)S(1)}) all-reduce(s32[4]{0:T(128)S(1)} %dynamic-update-slice.1, s32[112]{0:T(128)S(1)} %dynamic-update-slice.2, s32[112]{0:T(128)S(1)} %dynamic-update-slice), channel_id=1, replica_groups=mesh['tok'=8,'layer'=4] {'layer'}, use_global_device_ids=true, to_apply=%add.1 | all-reduce | flops 228 | bytes 1824
  48.6 0.0 copy-done
  48.6 10.0 %all_gather.15 = bf16[1,48,5120]{2,1,0:T(8,128)(2,1)S(1)} all-gather(bf16[1,48,640]{2,1,0:T(8,128)(2,1)S(1)} %copy-done), channel_id=1, replica_groups=mesh['tok'=8,'layer'=4] {'tok'}, dimensions={2}, use_global_device_ids=true | all-gather | bytes 552960 | tf_op jit(solution)/shard_map/all_gather | solution.py:19
  58.6 0.1 select_reduce_fusion
  58.7 0.0 all-to-all-done
  58.7 0.3 squeeze.9
  59.0 0.5 fusion.10
  59.6 0.0 all-gather.2.cloned.1.call-done
  59.6 1.9 %multiply_reduce_fusion = (f32[112]{0:T(128)S(1)}, f32[112,128]{1,0:T(8,128)S(1)}) fusion(bf16[112,5120]{1,0:T(8,128)(2,1)S(1)} %squeeze.9, bf16[1,128,5120]{2,1,0:T(8,128)(2,1)} %all-gather.2.cloned.1.call-done), kind=kOutput, calls=%fused_computation.11 | convolution fusion | flops 146829200 | bytes 2515392 | tf_op jit(solution)/shard_map/dot_general | solution.py:8
  61.6 0.1 copy.14
  61.7 0.1 multiply_convert_fusion
  61.8 2.5 %fusion.4 = f32[176,5120]{1,0:T(8,128)} fusion(bf16[112,5120]{1,0:T(8,128)(2,1)S(1)} %squeeze.9, bf16[112,128]{1,0:T(8,128)(2,1)S(1)} %multiply_convert_fusion, bf16[112,48]{1,0:T(8,128)(2,1)S(1)} %copy.14), kind=kOutput, calls=%fused_computation.6 | convolution fusion | flops 201929728 | bytes 4790784 | tf_op jit(solution)/shard_map/dot_general | solution.py:49
  64.3 0.0 reduce-scatter.2.cloned.1.call-update
  64.3 46.9 %reduce-scatter.2.cloned.1.call-done = f32[176,640]{1,0:T(8,128)} async-done(((f32[176,5120]{1,0:T(8,128)}), f32[176,640]{1,0:T(8,128)}) %reduce-scatter.2.cloned.1.call-update) | async-done | bytes 450576 | tf_op jit(solution)/shard_map/reduce_scatter | solution.py:52
  111.2 1.6 %slice_bitcast_fusion.1 = f32[1,48,640]{2,1,0:T(8,128)} fusion(f32[176,640]{1,0:T(8,128)} %reduce-scatter.2.cloned.1.call-done), kind=kLoop, calls=%fused_computation.5 | loop fusion | bytes 245760 | tf_op jit(solution)/shard_map/broadcast_in_dim | solution.py:53
  112.8 1.7 %slice_bitcast_fusion = f32[1,128,640]{2,1,0:T(8,128)} fusion(f32[176,640]{1,0:T(8,128)} %reduce-scatter.2.cloned.1.call-done), kind=kLoop, calls=%fused_computation.4 | loop fusion | bytes 655360 | tf_op jit(solution)/shard_map/broadcast_in_dim | solution.py:53
  (7 shorter events, 0.1 us)
Async XLA Ops:
  7.2 52.4 %all-gather.2.cloned.1.call-start = ((), (), s32[]{:S(2)}) async-start(), calls=%async_computation.2 | async-start | bytes 1474560 | tf_op jit(solution)/shard_map/all_gather | solution.py:20
  10.6 7.2 %copy-start.3 = (u32[32]{0:T(128)S(1)}, u32[32]{0:T(128)}, u32[]{:S(2)}) copy-start(u32[32]{0:T(128)} %constant.35) | copy-start | bytes 388
  10.6 8.4 %copy-start.1 = (s32[28]{0:T(128)S(1)}, s32[28]{0:T(128)}, u32[]{:S(2)}) copy-start(s32[28]{0:T(128)} %param.10) | copy-start | bytes 340
  10.6 8.7 %copy-start.2 = (s32[28]{0:T(128)S(1)}, s32[28]{0:T(128)}, u32[]{:S(2)}) copy-start(s32[28]{0:T(128)} %param.9) | copy-start | bytes 340
  10.6 38.0 %copy-start = (bf16[1,48,640]{2,1,0:T(8,128)(2,1)S(1)}, bf16[1,48,640]{2,1,0:T(8,128)(2,1)}, u32[]{:S(2)}) copy-start(bf16[1,48,640]{2,1,0:T(8,128)(2,1)} %param.7) | copy-start | bytes 184324
  10.6 48.1 %all-to-all-start = ((bf16[4,28,5120]{2,1,0:T(8,128)(2,1)}), bf16[4,28,5120]{2,1,0:T(8,128)(2,1)S(1)}, u32[]{:S(2)}, u32[]{:S(2)}) async-start(bf16[4,28,5120]{2,1,0:T(8,128)(2,1)} %copy.13), calls=%async_computation | async-start | bytes 2621440 | tf_op jit(solution)/shard_map/all_to_all | solution.py:16
  17.1 94.1 %reduce-scatter.2.cloned.1.call-start = ((), (), s32[]{:S(2)}) async-start(), calls=%async_computation.3 | async-start | bytes 4055040 | tf_op jit(solution)/shard_map/reduce_scatter | solution.py:52
Sparse Core Ops, SparseCore 0:
  9.9 27.1 all-gather.1
  64.4 46.7 reduce-scatter.1
where the time goes:
time: 122 us; the launch traced here: 121 us
  waiting for transfers between devices  47.6 us (39%)
  blocking collectives  38.3 us (31%)
  between operations  15.4 us (13%)
  local copies, waits for them, and re-layouts  8.21 us (7%)
  starting transfers between devices  6.53 us (5%)
  matrix products  4.97 us (4%)
    reduce_scatter x1, waiting for transfers between devices, local(): lax.psum_scatter(partial_value, 'tok', scatter_dimension=1, tiled=True)  46.9 us
    unnamed x1, blocking collectives  28.4 us
    all_gather x1, blocking collectives, local(): lax.all_gather(pos_weight, 'tok', axis=2, tiled=True)  9.97 us
    all_to_all x1, starting transfers between devices, local(): lax.all_to_all(activations, 'layer', split_axis=0, concat_axis=1, tiled=T...  6.49 us
    unnamed x16, local copies, waits for them, and re-layouts  4.53 us
    broadcast_in_dim x2, local copies, waits for them, and re-layouts, local(): return (summed[None, :tag_count], summed[None, tag_count:])  3.27 us
    dot_general x1, matrix products, local(): lax.dot_general(joined, owned_rows, (((0,), (0,)), ((), ())), preferred_e...  2.5 us
    dot_general x2, matrix products, contract(): lax.dot_general(left, right, (((1,), (1,)), ((), ())), preferred_element_...  2.47 us
  transfers between devices with their start and end apart: 3, of which 1 were waited for; matrix products, arithmetic and copies ran while one was open for 5% of the time, Pallas kernels for 0%

commit v1 on v0

--- a/solution.py
+++ b/solution.py
@@ -16,7 +16,7 @@
     owned_rows = lax.all_to_all(activations, "layer", split_axis=0, concat_axis=1, tiled=True)[0]
     row_count = owned_rows.shape[0]
     pos_full, depth_full = (
-        lax.all_gather(pos_weight, "tok", axis=2, tiled=True),
+        jnp.concatenate(lax.all_gather(pos_weight, "tok"), axis=2),
         lax.all_gather(depth_weight, "tok", axis=2, tiled=True),
     )
     logits = contract(owned_rows, pos_full[0])

time: 122 us -> 122 us (level)
    unnamed x16 -> x17, local copies, waits for them, and re-layouts: 4.53 us -> 4.57 us
where the time goes in v1:
time: 122 us; the launch traced here: 121 us
  waiting for transfers between devices  47.6 us (39%)
  blocking collectives  38.2 us (31%)
  between operations  15.4 us (13%)
  local copies, waits for them, and re-layouts  8.25 us (7%)
  starting transfers between devices  6.53 us (5%)
  matrix products  4.97 us (4%)
    reduce_scatter x1, waiting for transfers between devices, local(): lax.psum_scatter(partial_value, 'tok', scatter_dimension=1, tiled=True)  46.9 us
    unnamed x1, blocking collectives  28.4 us
    all_gather x1, blocking collectives, local(): lax.all_gather(pos_weight, 'tok')  9.84 us
    all_to_all x1, starting transfers between devices, local(): lax.all_to_all(activations, 'layer', split_axis=0, concat_axis=1, tiled=T...  6.49 us
    unnamed x17, local copies, waits for them, and re-layouts  4.57 us
    broadcast_in_dim x2, local copies, waits for them, and re-layouts, local(): return (summed[None, :tag_count], summed[None, tag_count:])  3.27 us
    dot_general x1, matrix products, local(): lax.dot_general(joined, owned_rows, (((0,), (0,)), ((), ())), preferred_e...  2.49 us
    dot_general x2, matrix products, contract(): lax.dot_general(left, right, (((1,), (1,)), ((), ())), preferred_element_...  2.47 us
  transfers between devices with their start and end apart: 3, of which 1 were waited for; matrix products, arithmetic and copies ran while one was open for 5% of the time, Pallas kernels for 0%

profile of v1, /device:TPU:0, one launch (start us, length us, event | category | flops | bytes accessed | tf_op | source)
XLA Modules:
  0.0 121.2 jit_solution(9883093201118089357)
XLA Ops:
  7.2 0.0 all-gather.3.cloned.1.call-start
  7.2 0.7 all-gather.3.cloned.1.call-update
  7.9 2.7 %copy.15 = bf16[4,28,5120]{2,1,0:T(8,128)(2,1)} copy(bf16[4,28,5120]{2,0,1:T(4,128)(2,1)} %param.6) | data formatting | bytes 2293760 | tf_op args[0]
  10.6 0.0 copy-start.3
  10.6 0.0 copy-start.1
  10.6 0.0 copy-start.2
  10.6 0.0 copy-start
  10.6 6.5 %all-to-all-start = ((bf16[4,28,5120]{2,1,0:T(8,128)(2,1)}), bf16[4,28,5120]{2,1,0:T(8,128)(2,1)S(1)}, u32[]{:S(2)}, u32[]{:S(2)}) async-start(bf16[4,28,5120]{2,1,0:T(8,128)(2,1)} %copy.15), calls=%async_computation | async-start | bytes 2621440 | tf_op jit(solution)/shard_map/all_to_all | solution.py:16
  17.1 0.0 reduce-scatter.2.cloned.1.call-start
  17.8 0.0 copy-done.3
  17.8 0.6 dynamic-slice
  19.0 0.0 copy-done.1
  19.0 0.2 dynamic-update-slice.2
  19.3 0.0 copy-done.2
  19.3 0.2 dynamic-update-slice
  19.5 0.8 dynamic-update-slice.1
  20.3 28.4 %all-reduce.3 = (s32[4]{0:T(128)S(1)}, s32[112]{0:T(128)S(1)}, s32[112]{0:T(128)S(1)}) all-reduce(s32[4]{0:T(128)S(1)} %dynamic-update-slice.1, s32[112]{0:T(128)S(1)} %dynamic-update-slice.2, s32[112]{0:T(128)S(1)} %dynamic-update-slice), channel_id=1, replica_groups=mesh['tok'=8,'layer'=4] {'layer'}, use_global_device_ids=true, to_apply=%add.1 | all-reduce | flops 228 | bytes 1824
  48.6 0.0 copy-done
  48.6 9.8 %all-gather = bf16[8,48,640]{2,1,0:T(8,128)(2,1)S(1)} all-gather(bf16[1,48,640]{2,1,0:T(8,128)(2,1)S(1)} %copy-done), channel_id=2, replica_groups=mesh['tok'=8,'layer'=4] {'tok'}, dimensions={0}, use_global_device_ids=true | all-gather | bytes 552960 | tf_op jit(solution)/shard_map/all_gather | solution.py:19
  58.5 0.1 select_reduce_fusion
  58.6 0.0 all-to-all-done
  58.6 0.3 squeeze.6
  58.9 0.5 fusion.8
  59.5 0.0 all-gather.3.cloned.1.call-done
  59.5 1.9 %multiply_reduce_fusion = (f32[112]{0:T(128)S(1)}, f32[112,128]{1,0:T(8,128)S(1)}) fusion(bf16[112,5120]{1,0:T(8,128)(2,1)S(1)} %squeeze.6, bf16[1,128,5120]{2,1,0:T(8,128)(2,1)} %all-gather.3.cloned.1.call-done), kind=kOutput, calls=%fused_computation.9 | convolution fusion | flops 146829200 | bytes 2515392 | tf_op jit(solution)/shard_map/dot_general | solution.py:8
  61.5 0.1 copy.17
  61.6 0.1 multiply_convert_fusion
  61.7 2.5 %fusion.2 = f32[176,5120]{1,0:T(8,128)} fusion(bf16[112,5120]{1,0:T(8,128)(2,1)S(1)} %squeeze.6, bf16[112,128]{1,0:T(8,128)(2,1)S(1)} %multiply_convert_fusion, bf16[112,48]{1,0:T(8,128)(2,1)S(1)} %copy.17), kind=kOutput, calls=%fused_computation.4 | convolution fusion | flops 201929728 | bytes 4790784 | tf_op jit(solution)/shard_map/dot_general | solution.py:49
  64.2 0.0 reduce-scatter.2.cloned.1.call-update
  64.2 46.9 %reduce-scatter.2.cloned.1.call-done = f32[176,640]{1,0:T(8,128)} async-done(((f32[176,5120]{1,0:T(8,128)}), f32[176,640]{1,0:T(8,128)}) %reduce-scatter.2.cloned.1.call-update) | async-done | bytes 450576 | tf_op jit(solution)/shard_map/reduce_scatter | solution.py:52
  111.1 1.6 %slice_bitcast_fusion.1 = f32[1,48,640]{2,1,0:T(8,128)} fusion(f32[176,640]{1,0:T(8,128)} %reduce-scatter.2.cloned.1.call-done), kind=kLoop, calls=%fused_computation.3 | loop fusion | bytes 245760 | tf_op jit(solution)/shard_map/broadcast_in_dim | solution.py:53
  112.7 1.7 %slice_bitcast_fusion = f32[1,128,640]{2,1,0:T(8,128)} fusion(f32[176,640]{1,0:T(8,128)} %reduce-scatter.2.cloned.1.call-done), kind=kLoop, calls=%fused_computation.2 | loop fusion | bytes 655360 | tf_op jit(solution)/shard_map/broadcast_in_dim | solution.py:53
  (8 shorter events, 0.1 us)
Async XLA Ops:
  7.2 52.4 %all-gather.3.cloned.1.call-start = ((), (), s32[]{:S(2)}) async-start(), calls=%async_computation.2 | async-start | bytes 1474560 | tf_op jit(solution)/shard_map/all_gather | solution.py:20
  10.6 7.2 %copy-start.3 = (u32[32]{0:T(128)S(1)}, u32[32]{0:T(128)}, u32[]{:S(2)}) copy-start(u32[32]{0:T(128)} %constant.35) | copy-start | bytes 388
  10.6 8.4 %copy-start.1 = (s32[28]{0:T(128)S(1)}, s32[28]{0:T(128)}, u32[]{:S(2)}) copy-start(s32[28]{0:T(128)} %param.10) | copy-start | bytes 340
  10.6 8.7 %copy-start.2 = (s32[28]{0:T(128)S(1)}, s32[28]{0:T(128)}, u32[]{:S(2)}) copy-start(s32[28]{0:T(128)} %param.9) | copy-start | bytes 340
  10.6 38.0 %copy-start = (bf16[1,48,640]{2,1,0:T(8,128)(2,1)S(1)}, bf16[1,48,640]{2,1,0:T(8,128)(2,1)}, u32[]{:S(2)}) copy-start(bf16[1,48,640]{2,1,0:T(8,128)(2,1)} %param.7) | copy-start | bytes 184324
  10.6 48.0 %all-to-all-start = ((bf16[4,28,5120]{2,1,0:T(8,128)(2,1)}), bf16[4,28,5120]{2,1,0:T(8,128)(2,1)S(1)}, u32[]{:S(2)}, u32[]{:S(2)}) async-start(bf16[4,28,5120]{2,1,0:T(8,128)(2,1)} %copy.15), calls=%async_computation | async-start | bytes 2621440 | tf_op jit(solution)/shard_map/all_to_all | solution.py:16
  17.1 94.0 %reduce-scatter.2.cloned.1.call-start = ((), (), s32[]{:S(2)}) async-start(), calls=%async_computation.3 | async-start | bytes 4055040 | tf_op jit(solution)/shard_map/reduce_scatter | solution.py:52
Sparse Core Ops, SparseCore 0:
  9.9 27.1 all-gather.2
  64.4 46.7 reduce-scatter.1
